TPU v7x, 32 devices: a whole 2x2x4 slice. The times are simulated.
32 devices in a mesh: tensor: 8 (over z, x), expert: 2 (over core), dp: 2 (over y).
Axes of the slice: x: 2, y: 2, z: 4, core: 2. Of those that a mesh axis runs over, the one named last changes fastest.
Arguments:
- tokens: bfloat16 [512, 2048], P(('expert', 'dp')), may hold values from -6 to 6
- tangent: bfloat16 [512, 2048], P(('expert', 'dp')), may hold values from -6 to 6
- cotangent: bfloat16 [512, 2048], P(('expert', 'dp')), may hold values from -0.59765625 to 0.59765625
- expert_ids: int32 [512, 8], P(('expert', 'dp')), may hold values from 0 to 15, all different within a row; in each aligned block of 128 rows (0 to 127, 128 to 255, ...) at most 96 rows name the same one
- gates: float32 [512, 8], P(('expert', 'dp')), may hold values from 0.1 to 1
- w_in: bfloat16 [16, 2, 768, 2048], P(('tensor', 'expert'), None, None, 'dp'), may hold values from -0.125 to 0.125
- v_in: bfloat16 [16, 2, 768, 2048], P(('tensor', 'expert'), None, None, 'dp'), may hold values from -0.125 to 0.125
- w_out: bfloat16 [16, 768, 2048], P(('tensor', 'expert'), None, 'dp'), may hold values from -0.21875 to 0.21875
- v_out: bfloat16 [16, 768, 2048], P(('tensor', 'expert'), None, 'dp'), may hold values from -0.21875 to 0.21875
Outputs:
- hvp_tokens: float32 [512, 2048], P(('expert', 'dp'))
- hvp_in: float32 [16, 2, 768, 2048], P(('tensor', 'expert'), None, None, 'dp')
- hvp_out: float32 [16, 768, 2048], P(('tensor', 'expert'), None, 'dp')
Inputs may be any that keep to these rules, and one draw needn't show every extreme that they name: `expert_ids`: each token names 8 different experts; among the tokens of one block of 128 no expert is named more than 96 times, and some expert reaches 96 in some blocks.
All inputs are finite; a program needn't handle non-finite values.
Results may differ from a plain program's by a relative error of at most 0.013.
Values may be sent and summed in bfloat16 or wider, within the bound.
A program may use at most 128 MiB of HBM per device.

v0:
```python
import jax
import jax.numpy as jnp
from jax import lax
from jax.sharding import PartitionSpec as P


def expert_terms(rows_x, rows_u, rows_dy, w_in, v_in, w_out, v_out):
    f32 = jnp.float32
    pre = jnp.einsum("nesd,egfd->nesgf", rows_x, w_in, preferred_element_type=f32)
    pre_dot = jnp.einsum("nesd,egfd->nesgf", rows_u, w_in, preferred_element_type=f32)
    pre_dot = pre_dot + jnp.einsum("nesd,egfd->nesgf", rows_x, v_in, preferred_element_type=f32)
    gate_pre, up_val = (pre[:, :, :, 0], pre[:, :, :, 1])
    gate_dot, up_dot = (pre_dot[:, :, :, 0], pre_dot[:, :, :, 1])
    back = jnp.einsum("nesd,efd->nesf", rows_dy, w_out, preferred_element_type=f32)
    back_dot = jnp.einsum("nesd,efd->nesf", rows_dy, v_out, preferred_element_type=f32)
    sigma = jax.nn.sigmoid(gate_pre)
    silu_val = gate_pre * sigma
    first = sigma * (1.0 + gate_pre * (1.0 - sigma))
    second = sigma * (1.0 - sigma) * (2.0 + gate_pre * (1.0 - 2.0 * sigma))
    grad_a = back * up_val * first
    grad_b = back * silu_val
    tang_a = back_dot * up_val * first + back * up_dot * first + back * up_val * second * gate_dot
    tang_b = back_dot * silu_val + back * first * gate_dot
    grads = jnp.stack([grad_a, grad_b], axis=3).astype(jnp.bfloat16)
    tangs = jnp.stack([tang_a, tang_b], axis=3).astype(jnp.bfloat16)
    hidden_dot = (first * gate_dot * up_val + silu_val * up_dot).astype(jnp.bfloat16)
    partial_value = jnp.einsum("nesgf,egfd->nesd", tangs, w_in, preferred_element_type=f32)
    partial_value = partial_value + jnp.einsum(
        "nesgf,egfd->nesd", grads, v_in, preferred_element_type=f32
    )
    part_in = jnp.einsum("nesd,nesgf->egfd", rows_u, grads, preferred_element_type=f32)
    part_in = part_in + jnp.einsum("nesd,nesgf->egfd", rows_x, tangs, preferred_element_type=f32)
    part_out = jnp.einsum("nesf,nesd->efd", hidden_dot, rows_dy, preferred_element_type=f32)
    return (partial_value.astype(jnp.bfloat16), part_in, part_out)


def shards(tokens, tangent, cotangent, expert_ids, gates, w_in, v_in, w_out, v_out):
    n_tensor = lax.axis_size("tensor")
    n_expert = lax.axis_size("expert")
    rank = lax.axis_index("tensor")
    local_experts = w_in.shape[0]
    all_experts = local_experts * n_tensor * n_expert
    tok_rows, width = tokens.shape
    topk = expert_ids.shape[1]
    share = min(tok_rows // n_tensor, 3 * tok_rows * topk // (2 * all_experts * n_tensor))
    full_in, full_v_in, full_out, full_v_out = (
        lax.all_gather(w_in, "dp", axis=3, tiled=True),
        lax.all_gather(v_in, "dp", axis=3, tiled=True),
        lax.all_gather(w_out, "dp", axis=2, tiled=True),
        lax.all_gather(v_out, "dp", axis=2, tiled=True),
    )
    picks = expert_ids.reshape(-1)
    onehot = (picks[:, None] == jnp.arange(all_experts, dtype=jnp.int32)[None, :]).astype(jnp.int32)
    running = jnp.cumsum(onehot, axis=0) - 1
    slots = jnp.sum(onehot * running, axis=1)
    owned = slots // share == rank
    limit = all_experts * share
    target = jnp.where(owned, picks * share + slots % share, limit)
    scale = gates.reshape(-1)
    rows_x = jnp.repeat(tokens, topk, axis=0)
    rows_u = jnp.repeat(tangent, topk, axis=0)
    rows_dy = (scale[:, None] * jnp.repeat(cotangent, topk, axis=0).astype(jnp.float32)).astype(
        jnp.bfloat16
    )
    empty = jnp.zeros((limit, width), jnp.bfloat16)
    wide_shape = (n_tensor * n_expert, local_experts, share, width)
    send_x = empty.at[target].set(rows_x, mode="drop").reshape(wide_shape)
    send_u = empty.at[target].set(rows_u, mode="drop").reshape(wide_shape)
    send_dy = empty.at[target].set(rows_dy, mode="drop").reshape(wide_shape)
    got_x, got_u, got_dy = (
        lax.all_to_all(send_x, ("tensor", "expert"), split_axis=0, concat_axis=0, tiled=True),
        lax.all_to_all(send_u, ("tensor", "expert"), split_axis=0, concat_axis=0, tiled=True),
        lax.all_to_all(send_dy, ("tensor", "expert"), split_axis=0, concat_axis=0, tiled=True),
    )
    partial_value, part_in, part_out = expert_terms(
        got_x, got_u, got_dy, full_in, full_v_in, full_out, full_v_out
    )
    returned = lax.all_to_all(
        partial_value, ("tensor", "expert"), split_axis=0, concat_axis=0, tiled=True
    )
    table = returned.astype(jnp.float32).reshape(limit, width)
    picked = table[jnp.minimum(target, limit - 1)]
    picked = jnp.where(owned[:, None], picked, 0.0)
    own_sums = jnp.sum(picked.reshape(tok_rows, topk, width), axis=1)
    hvp_tokens = lax.psum(own_sums.astype(jnp.bfloat16), "tensor").astype(jnp.float32)
    hvp_in, hvp_out = (
        lax.psum_scatter(
            part_in.astype(jnp.bfloat16), "dp", scatter_dimension=3, tiled=True
        ).astype(jnp.float32),
        lax.psum_scatter(
            part_out.astype(jnp.bfloat16), "dp", scatter_dimension=2, tiled=True
        ).astype(jnp.float32),
    )
    return (hvp_tokens, hvp_in, hvp_out)


def solution(mesh):
    placed = (
        P(("expert", "dp"), None),
        P(("expert", "dp"), None),
        P(("expert", "dp"), None),
        P(("expert", "dp"), None),
        P(("expert", "dp"), None),
        P(("tensor", "expert"), None, None, "dp"),
        P(("tensor", "expert"), None, None, "dp"),
        P(("tensor", "expert"), None, "dp"),
        P(("tensor", "expert"), None, "dp"),
    )
    return jax.shard_map(
        shards,
        mesh=mesh,
        in_specs=placed,
        out_specs=(
            P(("expert", "dp"), None),
            P(("tensor", "expert"), None, None, "dp"),
            P(("tensor", "expert"), None, "dp"),
        ),
        check_vma=False,
    )
```

profile of v0, /device:TPU:0, one launch (start us, length us, event | category | flops | bytes accessed | tf_op | source)
XLA Modules:
  0.0 534.4 jit_solution(1958558635749751632)
XLA Ops:
  7.2 0.7 all-gather.5.cloned.1.call-update
  8.0 0.7 all-gather.7.cloned.1.call-update
  8.7 0.7 all-gather.11.cloned.1.call-update
  9.4 0.1 copy.34
  9.7 0.1 copy.38
  10.0 4.5 reduce-window.6
  14.6 0.1 copy.36
  15.0 6.5 %scatter_custom_fusion.1 = bf16[192,2048]{1,0:T(8,128)(2,1)S(1)} fusion(s32[1024]{0:T(1024)S(1)} %bitcast.255, bf16[128,2048]{1,0:T(8,128)(2,1)S(1)} %copy-done, bf16[]{:T(256)} %constant.42.clone.1), kind=kCustom, calls=%fused_computation.25 | custom fusion | bytes 1310722 | tf_op jit(solution)/shard_map/scatter | solution.py:67
  21.6 1.1 reshape.381
  22.7 7.4 %all-to-all-start.1 = ((bf16[16,1,12,2048]{3,2,1,0:T(8,128)(2,1)}), bf16[16,1,12,2048]{3,2,1,0:T(8,128)(2,1)S(1)}, u32[]{:S(2)}, u32[]{:S(2)}) async-start(bf16[16,1,12,2048]{3,2,1,0:T(8,128)(2,1)} %bitcast.14), calls=%async_computation.1 | async-start | bytes 2097152 | tf_op jit(solution)/shard_map/all_to_all | solution.py:71
  30.1 0.1 copy.39
  30.3 0.1 convert_element_type.72
  30.5 6.9 %scatter_custom_fusion = bf16[192,2048]{1,0:T(8,128)(2,1)S(1)} fusion(s32[1024]{0:T(1024)S(1)} %bitcast.256, f32[128,2048]{1,0:T(8,128)S(1)} %convert_element_type.72, f32[1024]{0:T(1024)S(1)} %mul.184, bf16[]{:T(256)} %constant.42.clone.1), kind=kCustom, calls=%fused_computation.22 | custom fusion | flops 4194304 | bytes 1839106 | tf_op jit(solution)/shard_map/scatter | solution.py:69
  37.4 1.1 reshape.377
  38.6 14.5 %all-to-all-done.1 = bf16[16,1,12,2048]{3,2,1,0:T(8,128)(2,1)S(1)} async-done(((bf16[16,1,12,2048]{3,2,1,0:T(8,128)(2,1)}), bf16[16,1,12,2048]{3,2,1,0:T(8,128)(2,1)S(1)}, u32[]{:S(2)}, u32[]{:S(2)}) %all-to-all-start.1) | async-done | bytes 786464 | tf_op jit(solution)/shard_map/all_to_all | solution.py:71
  53.0 6.8 %all-to-all-start = ((bf16[16,1,12,2048]{3,2,1,0:T(8,128)(2,1)}), bf16[16,1,12,2048]{3,2,1,0:T(8,128)(2,1)S(1)}, u32[]{:S(2)}, u32[]{:S(2)}) async-start(bf16[16,1,12,2048]{3,2,1,0:T(8,128)(2,1)} %bitcast.6), calls=%async_computation | async-start | bytes 2097152 | tf_op jit(solution)/shard_map/all_to_all | solution.py:73
  59.8 0.2 all-gather.9.cloned.1.call-start
  60.0 0.3 all-gather.9.cloned.1.call-update
  60.4 6.5 %scatter_custom_fusion.2 = bf16[192,2048]{1,0:T(8,128)(2,1)S(1)} fusion(s32[1024]{0:T(1024)S(1)} %bitcast.257, bf16[128,2048]{1,0:T(8,128)(2,1)S(1)} %copy-done.9, bf16[]{:T(256)} %constant.42.clone.1), kind=kCustom, calls=%fused_computation.23 | custom fusion | bytes 1310722 | tf_op jit(solution)/shard_map/scatter | solution.py:68
  66.9 1.1 reshape.386
  68.1 14.6 %all-to-all-done = bf16[16,1,12,2048]{3,2,1,0:T(8,128)(2,1)S(1)} async-done(((bf16[16,1,12,2048]{3,2,1,0:T(8,128)(2,1)}), bf16[16,1,12,2048]{3,2,1,0:T(8,128)(2,1)S(1)}, u32[]{:S(2)}, u32[]{:S(2)}) %all-to-all-start) | async-done | bytes 786464 | tf_op jit(solution)/shard_map/all_to_all | solution.py:73
  82.7 6.8 %all-to-all-start.2 = ((bf16[16,1,12,2048]{3,2,1,0:T(8,128)(2,1)}), bf16[16,1,12,2048]{3,2,1,0:T(8,128)(2,1)S(1)}, u32[]{:S(2)}, u32[]{:S(2)}) async-start(bf16[16,1,12,2048]{3,2,1,0:T(8,128)(2,1)} %bitcast.30), calls=%async_computation.2 | async-start | bytes 2097152 | tf_op jit(solution)/shard_map/all_to_all | solution.py:72
  89.5 3.3 fusion.53
  92.9 46.3 %all-gather.7.cloned.1.call-done = bf16[1,2,768,2048]{3,2,1,0:T(8,128)(2,1)} async-done(((bf16[1,2,768,1024]{3,2,1,0:T(8,128)(2,1)}), bf16[1,2,768,2048]{3,2,1,0:T(8,128)(2,1)}) %all-gather.7.cloned.1.call-update) | async-done | bytes 6291472 | tf_op jit(solution)/shard_map/all_gather | solution.py:47
  139.1 6.4 %fusion.44 = f32[16,1,12,2,768]{4,0,2,3,1:T(8,128)} fusion(bf16[1,2,768,2048]{3,2,1,0:T(8,128)(2,1)} %all-gather.7.cloned.1.call-done, bf16[16,1,12,2048]{3,2,1,0:T(8,128)(2,1)} %copy-done.6), kind=kOutput, calls=%fused_computation.41 | convolution fusion | flops 1207959552 | bytes 8257536 | tf_op jit(solution)/shard_map/nesd,egfd->nesgf/dot_general | solution.py:9
  145.6 75.5 %all-gather.11.cloned.1.call-done = bf16[1,2,768,2048]{3,2,1,0:T(8,128)(2,1)} async-done(((bf16[1,2,768,1024]{3,2,1,0:T(8,128)(2,1)}), bf16[1,2,768,2048]{3,2,1,0:T(8,128)(2,1)}) %all-gather.11.cloned.1.call-update) | async-done | bytes 6291472 | tf_op jit(solution)/shard_map/all_gather | solution.py:48
  221.1 6.4 %fusion.6 = f32[16,12,2,768]{3,0,1,2:T(8,128)} fusion(bf16[1,2,768,2048]{3,2,1,0:T(8,128)(2,1)} %all-gather.11.cloned.1.call-done, bf16[16,1,12,2048]{3,2,1,0:T(8,128)(2,1)} %copy-done.6), kind=kOutput, calls=%fused_computation.14 | convolution fusion | flops 1207959552 | bytes 8257536 | tf_op jit(solution)/shard_map/nesd,egfd->nesgf/dot_general | solution.py:11
  227.5 7.6 %fusion.50 = f32[16,1,12,2,768]{4,0,2,3,1:T(8,128)} fusion(f32[16,12,2,768]{3,0,1,2:T(8,128)} %fusion.6, bf16[1,2,768,2048]{3,2,1,0:T(8,128)(2,1)} %all-gather.7.cloned.1.call-done, bf16[16,1,12,2048]{3,2,1,0:T(8,128)(2,1)S(1)} %all-to-all-done.2), kind=kOutput, calls=%fused_computation.43 | convolution fusion | flops 1208254464 | bytes 9437184 | tf_op jit(solution)/shard_map/nesd,egfd->nesgf/dot_general | solution.py:10
  235.1 32.3 %all-gather.9.cloned.1.call-done = bf16[1,768,2048]{2,1,0:T(8,128)(2,1)} async-done(((bf16[1,768,1024]{2,1,0:T(8,128)(2,1)}), bf16[1,768,2048]{2,1,0:T(8,128)(2,1)}) %all-gather.9.cloned.1.call-update) | async-done | bytes 3145744 | tf_op jit(solution)/shard_map/all_gather | solution.py:49
  267.4 4.5 fusion.94
  272.0 4.5 fusion.27
  276.6 1.5 fusion.39
  278.1 1.4 copy.48
  279.5 5.6 %all-to-all-start.3 = ((bf16[16,1,12,2048]{3,2,1,0:T(8,128)(2,1)}), bf16[16,1,12,2048]{3,2,1,0:T(8,128)(2,1)S(1)}, u32[]{:S(2)}, u32[]{:S(2)}) async-start(bf16[16,1,12,2048]{3,2,1,0:T(8,128)(2,1)} %copy.48), calls=%async_computation.3 | async-start | bytes 2097152 | tf_op jit(solution)/shard_map/all_to_all | solution.py:78
  285.1 0.3 all-reduce.2.cloned.1.call-start
  285.6 22.4 %all-to-all-done.3 = bf16[16,1,12,2048]{3,2,1,0:T(8,128)(2,1)S(1)} async-done(((bf16[16,1,12,2048]{3,2,1,0:T(8,128)(2,1)}), bf16[16,1,12,2048]{3,2,1,0:T(8,128)(2,1)S(1)}, u32[]{:S(2)}, u32[]{:S(2)}) %all-to-all-start.3) | async-done | bytes 786464 | tf_op jit(solution)/shard_map/all_to_all | solution.py:78
  308.0 0.2 reshape.392
  308.2 6.9 %gather_fusion = f32[1024,2048]{1,0:T(8,128)} fusion(f32[192,2048]{1,0:T(8,128)S(1)} %reshape.392, s32[1024]{0:T(1024)S(1)} %broadcast_clamp_fusion), kind=kCustom, calls=%fused_computation | custom fusion | bytes 16781312 | tf_op jit(solution)/shard_map/gather | solution.py:82
  315.1 7.7 %fusion.1 = bf16[128,2048]{1,0:T(8,128)(2,1)} fusion(f32[1024,2048]{1,0:T(8,128)} %gather_fusion, pred[128,8]{1,0:T(8,128)(4,1)S(1)} %fusion.99), kind=kLoop, calls=%fused_computation.7 | loop fusion | flops 3932160 | bytes 8913920 | tf_op jit(solution)/shard_map/reduce_sum | solution.py:84
  322.9 4.7 fusion.26
  327.7 1.9 fusion.59
  329.7 4.8 fusion.3
  334.6 62.3 %all-reduce.2.cloned.1.call-done = bf16[128,2048]{1,0:T(8,128)(2,1)} async-done(((bf16[128,2048]{1,0:T(8,128)(2,1)}), bf16[128,2048]{1,0:T(8,128)(2,1)}) %all-reduce.2.cloned.1.call-update) | async-done | bytes 524304 | tf_op jit(solution)/shard_map/psum | solution.py:85
  396.9 2.1 convert_element_type.80
  399.0 43.2 %reduce-scatter.5.cloned.1.call-done = bf16[1,768,1024]{2,1,0:T(8,128)(2,1)} async-done(((bf16[1,768,2048]{2,1,0:T(8,128)(2,1)}), bf16[1,768,1024]{2,1,0:T(8,128)(2,1)}) %reduce-scatter.5.cloned.1.call-update) | async-done | bytes 1572880 | tf_op jit(solution)/shard_map/reduce_scatter | solution.py:90
  442.2 3.5 convert_element_type.88
  445.7 76.5 %reduce-scatter.3.cloned.1.call-done = bf16[1,2,768,1024]{3,2,1,0:T(8,128)(2,1)} async-done(((bf16[1,2,768,2048]{3,2,1,0:T(8,128)(2,1)}), bf16[1,2,768,1024]{3,2,1,0:T(8,128)(2,1)}) %reduce-scatter.3.cloned.1.call-update) | async-done | bytes 3145744 | tf_op jit(solution)/shard_map/reduce_scatter | solution.py:87
  522.2 5.3 convert_element_type.83
  (71 shorter events, 1.3 us)
Async XLA Ops:
  7.2 7.9 %copy-start = (bf16[128,2048]{1,0:T(8,128)(2,1)S(1)}, bf16[128,2048]{1,0:T(8,128)(2,1)}, u32[]{:S(2)}) copy-start(bf16[128,2048]{1,0:T(8,128)(2,1)} %param.9) | copy-start | bytes 1572868
  7.2 2.3 copy-start.10
  7.2 82.3 %all-gather.5.cloned.1.call-start = ((), (), s32[]{:S(2)}) async-start(), calls=%async_computation.6 | async-start | bytes 4718592 | tf_op jit(solution)/shard_map/all_gather | solution.py:50
  7.9 131.2 %all-gather.7.cloned.1.call-start = ((), (), s32[]{:S(2)}) async-start(), calls=%async_computation.7 | async-start | bytes 9437184 | tf_op jit(solution)/shard_map/all_gather | solution.py:47
  8.7 21.4 %copy-start.11 = (f32[128,8]{0,1:T(8,128)S(1)}, f32[128,8]{0,1:T(8,128)}, u32[]{:S(2)}) copy-start(f32[128,8]{0,1:T(8,128)} %param.13) | copy-start | bytes 12292
  8.7 21.6 %copy-start.8 = (bf16[128,2048]{1,0:T(8,128)(2,1)S(1)}, bf16[128,2048]{1,0:T(8,128)(2,1)}, u32[]{:S(2)}) copy-start(bf16[128,2048]{1,0:T(8,128)(2,1)} %param.11) | copy-start | bytes 1572868
  8.7 212.4 %all-gather.11.cloned.1.call-start = ((), (), s32[]{:S(2)}) async-start(), calls=%async_computation.9 | async-start | bytes 9437184 | tf_op jit(solution)/shard_map/all_gather | solution.py:48
  22.7 30.3 %all-to-all-start.1 = ((bf16[16,1,12,2048]{3,2,1,0:T(8,128)(2,1)}), bf16[16,1,12,2048]{3,2,1,0:T(8,128)(2,1)S(1)}, u32[]{:S(2)}, u32[]{:S(2)}) async-start(bf16[16,1,12,2048]{3,2,1,0:T(8,128)(2,1)} %bitcast.14), calls=%async_computation.1 | async-start | bytes 2097152 | tf_op jit(solution)/shard_map/all_to_all | solution.py:71
  30.3 30.1 %copy-start.9 = (bf16[128,2048]{1,0:T(8,128)(2,1)S(1)}, bf16[128,2048]{1,0:T(8,128)(2,1)}, u32[]{:S(2)}) copy-start(bf16[128,2048]{1,0:T(8,128)(2,1)} %param.10) | copy-start | bytes 1572868
  53.0 29.7 %copy-start.6 = (bf16[16,1,12,2048]{3,2,1,0:T(8,128)(2,1)}, bf16[16,1,12,2048]{3,2,1,0:T(8,128)(2,1)S(1)}, u32[]{:S(2)}) copy-start(bf16[16,1,12,2048]{3,2,1,0:T(8,128)(2,1)S(1)} %all-to-all-done.1) | copy-start | bytes 2359300
  53.0 29.7 %all-to-all-start = ((bf16[16,1,12,2048]{3,2,1,0:T(8,128)(2,1)}), bf16[16,1,12,2048]{3,2,1,0:T(8,128)(2,1)S(1)}, u32[]{:S(2)}, u32[]{:S(2)}) async-start(bf16[16,1,12,2048]{3,2,1,0:T(8,128)(2,1)} %bitcast.6), calls=%async_computation | async-start | bytes 2097152 | tf_op jit(solution)/shard_map/all_to_all | solution.py:73
  59.8 207.6 %all-gather.9.cloned.1.call-start = ((), (), s32[]{:S(2)}) async-start(), calls=%async_computation.8 | async-start | bytes 4718592 | tf_op jit(solution)/shard_map/all_gather | solution.py:49
  82.7 184.7 %copy-start.4 = (bf16[16,1,12,2048]{3,2,1,0:T(8,128)(2,1)}, bf16[16,1,12,2048]{3,2,1,0:T(8,128)(2,1)S(1)}, u32[]{:S(2)}) copy-start(bf16[16,1,12,2048]{3,2,1,0:T(8,128)(2,1)S(1)} %all-to-all-done) | copy-start | bytes 2359300
  82.7 144.8 %all-to-all-start.2 = ((bf16[16,1,12,2048]{3,2,1,0:T(8,128)(2,1)}), bf16[16,1,12,2048]{3,2,1,0:T(8,128)(2,1)S(1)}, u32[]{:S(2)}, u32[]{:S(2)}) async-start(bf16[16,1,12,2048]{3,2,1,0:T(8,128)(2,1)} %bitcast.30), calls=%async_computation.2 | async-start | bytes 2097152 | tf_op jit(solution)/shard_map/all_to_all | solution.py:72
  227.5 7.6 %copy-start.2 = (bf16[16,1,12,2048]{3,2,1,0:T(8,128)(2,1)}, bf16[16,1,12,2048]{3,2,1,0:T(8,128)(2,1)S(1)}, u32[]{:S(2)}) copy-start(bf16[16,1,12,2048]{3,2,1,0:T(8,128)(2,1)S(1)} %all-to-all-done.2) | copy-start | bytes 2359300
  267.4 9.1 %slice-start = ((s8[6291456]{0:T(1024)(128)(4,1)}), s8[2097152]{0:T(1024)(128)(4,1)S(1)}, s32[]{:S(2)}) async-start(s8[6291456]{0:T(1024)(128)(4,1)} %bitcast.258), calls=%async_computation.13 | async-start | bytes 4194304
  272.0 4.6 copy-start.14
  272.0 4.6 copy-start.16
  272.0 4.6 copy-start.12
  272.0 4.6 slice-start.1
  279.5 28.5 %all-to-all-start.3 = ((bf16[16,1,12,2048]{3,2,1,0:T(8,128)(2,1)}), bf16[16,1,12,2048]{3,2,1,0:T(8,128)(2,1)S(1)}, u32[]{:S(2)}, u32[]{:S(2)}) async-start(bf16[16,1,12,2048]{3,2,1,0:T(8,128)(2,1)} %copy.48), calls=%async_computation.3 | async-start | bytes 2097152 | tf_op jit(solution)/shard_map/all_to_all | solution.py:78
  285.1 111.7 %all-reduce.2.cloned.1.call-start = ((), (), s32[]{:S(2)}) async-start(), calls=%async_computation.10 | async-start | bytes 1048576 | tf_op jit(solution)/shard_map/psum | solution.py:85
  315.1 7.8 %copy-start.5 = (bf16[16,1,12,2048]{3,2,1,0:T(8,128)(2,1)S(1)}, bf16[16,1,12,2048]{3,2,1,0:T(8,128)(2,1)}, u32[]{:S(2)}) copy-start(bf16[16,1,12,2048]{3,2,1,0:T(8,128)(2,1)} %copy-done.4) | copy-start | bytes 2359300
  322.8 4.9 copy-start.3
  322.8 4.9 copy-start.13
  322.8 119.3 %reduce-scatter.5.cloned.1.call-start = ((), (), s32[]{:S(2)}) async-start(), calls=%async_computation.12 | async-start | bytes 4718592 | tf_op jit(solution)/shard_map/reduce_scatter | solution.py:90
  327.6 2.0 copy-start.7
  327.6 2.0 copy-start.15
  327.7 2.0 copy-start.17
  327.7 194.5 %reduce-scatter.3.cloned.1.call-start = ((), (), s32[]{:S(2)}) async-start(), calls=%async_computation.11 | async-start | bytes 9437184 | tf_op jit(solution)/shard_map/reduce_scatter | solution.py:87
  442.2 85.4 %copy-start.1 = (bf16[128,2048]{1,0:T(8,128)(2,1)S(1)}, bf16[128,2048]{1,0:T(8,128)(2,1)}, u32[]{:S(2)}) copy-start(bf16[128,2048]{1,0:T(8,128)(2,1)} %param.9) | copy-start | bytes 1572868
Sparse Core Ops, SparseCore 0:
  9.5 47.6 all-gather.4
  58.8 80.3 all-gather.6
  140.7 80.3 all-gather.10
  222.5 44.8 all-gather.8
  322.9 73.8 all-reduce.1
  399.5 42.6 reduce-scatter.4
  445.1 77.1 reduce-scatter.2
where the time goes:
time: 535 us; the launch traced here: 534 us
  waiting for transfers between devices  390 us (73%)
  matrix products  45.7 us (9%)
  other arithmetic  30.5 us (6%)
  starting transfers between devices  27.3 us (5%)
  local copies, waits for them, and re-layouts  26.2 us (5%)
  between operations  14.6 us (3%)
    reduce_scatter x1, waiting for transfers between devices, shards(): lax.psum_scatter(part_in.astype(jnp.bfloat16), 'dp', scatter_dimension=3,...  76.5 us
    all_gather x1, waiting for transfers between devices, shards(): lax.all_gather(v_in, 'dp', axis=3, tiled=True)  75.5 us
    psum x1, waiting for transfers between devices, shards(): lax.psum(own_sums.astype(jnp.bfloat16), 'tensor').astype(jnp.float32)  62.3 us
    all_gather x1, waiting for transfers between devices, shards(): lax.all_gather(w_in, 'dp', axis=3, tiled=True)  46.3 us
    reduce_scatter x1, waiting for transfers between devices, shards(): lax.psum_scatter(part_out.astype(jnp.bfloat16), 'dp', scatter_dimension=2...  43.2 us
    all_gather x1, waiting for transfers between devices, shards(): lax.all_gather(w_out, 'dp', axis=2, tiled=True)  32.3 us
    all_to_all x1, waiting for transfers between devices, shards(): lax.all_to_all(partial_value, ('tensor', 'expert'), split_axis=0, concat_...  22.4 us
    all_to_all x1, waiting for transfers between devices, shards(): lax.all_to_all(send_dy, ('tensor', 'expert'), split_axis=0, concat_axis=0...  14.6 us
  transfers between devices with their start and end apart: 11, of which 9 were waited for; matrix products, arithmetic and copies ran while one was open for 13% of the time, Pallas kernels for 0%

commit v1 on v0

--- a/solution.py
+++ b/solution.py
@@ -1,7 +1,15 @@
+import functools
 import jax
 import jax.numpy as jnp
 from jax import lax
 from jax.sharding import PartitionSpec as P
+
+
+def close_the_samples_all(row_data, row_axis):
+    return jax.lax.all_gather(row_data, row_axis).sum(axis=0)
+
+
+assign_axis_part = functools.partial(close_the_samples_all, row_axis="tensor")
 
 
 def expert_terms(rows_x, rows_u, rows_dy, w_in, v_in, w_out, v_out):
@@ -82,7 +90,7 @@
     picked = table[jnp.minimum(target, limit - 1)]
     picked = jnp.where(owned[:, None], picked, 0.0)
     own_sums = jnp.sum(picked.reshape(tok_rows, topk, width), axis=1)
-    hvp_tokens = lax.psum(own_sums.astype(jnp.bfloat16), "tensor").astype(jnp.float32)
+    hvp_tokens = assign_axis_part(own_sums.astype(jnp.bfloat16)).astype(jnp.float32)
     hvp_in, hvp_out = (
         lax.psum_scatter(
             part_in.astype(jnp.bfloat16), "dp", scatter_dimension=3, tiled=True

time: 535 us -> 489 us (0.914)
  waiting for transfers between devices: 390 us -> 345 us
    all_gather x0 -> x1, waiting for transfers between devices: none -> 62.4 us  [close_the_samples_all(): return jax.lax.all_gather(row_data, row_axis).sum(axis=0)]
    psum x1 -> x0, waiting for transfers between devices: 62.3 us -> none  [shards(): lax.psum(own_sums.astype(jnp.bfloat16), 'tensor').astype(jnp.float32)]
    all_gather x1, waiting for transfers between devices: 46.3 us -> 2.89 us  [shards(): lax.all_gather(w_in, 'dp', axis=3, tiled=True)]
    reduce_scatter x1, waiting for transfers between devices: 43.2 us -> 0.02 us  [shards(): lax.psum_scatter(part_out.astype(jnp.bfloat16), 'dp', scatter_dimension=2...]
    all_gather x1, waiting for transfers between devices: 0.02 us -> 32.7 us  [shards(): lax.all_gather(v_out, 'dp', axis=2, tiled=True)]
    all_to_all x1, waiting for transfers between devices: 0.01 us -> 15.2 us  [shards(): lax.all_to_all(send_u, ('tensor', 'expert'), split_axis=0, concat_axis=0,...]
    all_to_all x1, waiting for transfers between devices: 14.6 us -> 0.01 us  [shards(): lax.all_to_all(send_dy, ('tensor', 'expert'), split_axis=0, concat_axis=0...]
    all_gather x1, waiting for transfers between devices: 32.3 us -> 43 us  [shards(): lax.all_gather(w_out, 'dp', axis=2, tiled=True)]
  transfers between devices with their start and end apart: 11 -> 11, of which waited for: 9 -> 9; matrix products, arithmetic and copies ran while one was open for 13% -> 20% of each run, Pallas kernels for 0% -> 0%
where the time goes in v1:
time: 489 us; the launch traced here: 488 us
  waiting for transfers between devices  345 us (71%)
  matrix products  42 us (9%)
  other arithmetic  32.5 us (7%)
  starting transfers between devices  27.2 us (6%)
  local copies, waits for them, and re-layouts  26.5 us (5%)
  between operations  14.5 us (3%)
    all_gather x1, waiting for transfers between devices, shards(): lax.all_gather(v_in, 'dp', axis=3, tiled=True)  75.5 us
    reduce_scatter x1, waiting for transfers between devices, shards(): lax.psum_scatter(part_in.astype(jnp.bfloat16), 'dp', scatter_dimension=3,...  74.5 us
    all_gather x1, waiting for transfers between devices, close_the_samples_all(): return jax.lax.all_gather(row_data, row_axis).sum(axis=0)  62.4 us
    all_gather x1, waiting for transfers between devices, shards(): lax.all_gather(w_out, 'dp', axis=2, tiled=True)  43 us
    all_gather x1, waiting for transfers between devices, shards(): lax.all_gather(v_out, 'dp', axis=2, tiled=True)  32.7 us
    all_to_all x1, waiting for transfers between devices, shards(): lax.all_to_all(partial_value, ('tensor', 'expert'), split_axis=0, concat_...  22.6 us
    all_to_all x1, waiting for transfers between devices, shards(): lax.all_to_all(send_u, ('tensor', 'expert'), split_axis=0, concat_axis=0,...  15.2 us
    all_to_all x1, waiting for transfers between devices, shards(): lax.all_to_all(send_x, ('tensor', 'expert'), split_axis=0, concat_axis=0,...  13.9 us
  transfers between devices with their start and end apart: 11, of which 9 were waited for; matrix products, arithmetic and copies ran while one was open for 20% of the time, Pallas kernels for 0%

profile of v1, /device:TPU:0, one launch (start us, length us, event | category | flops | bytes accessed | tf_op | source)
XLA Modules:
  0.0 487.9 jit_solution(8622860034079804569)
XLA Ops:
  7.2 0.7 all-gather.9.cloned.1.call-update
  8.0 0.7 all-gather.13.cloned.1.call-update
  8.7 0.7 all-gather.7.cloned.1.call-update
  9.4 0.1 copy.49
  9.7 4.5 reduce-window.6
  14.3 0.1 copy.51
  14.7 0.1 copy.53
  14.8 0.1 mul.183
  15.0 6.5 %scatter_custom_fusion.2 = bf16[192,2048]{1,0:T(8,128)(2,1)S(1)} fusion(s32[1024]{0:T(1024)S(1)} %bitcast.257, bf16[128,2048]{1,0:T(8,128)(2,1)S(1)} %copy-done, bf16[]{:T(256)} %constant.43.clone.1), kind=kCustom, calls=%fused_computation.23 | custom fusion | bytes 1310722 | tf_op jit(solution)/shard_map/scatter | solution.py:76
  21.6 1.1 reshape.394
  22.7 7.5 %all-to-all-start.2 = ((bf16[16,1,12,2048]{3,2,1,0:T(8,128)(2,1)}), bf16[16,1,12,2048]{3,2,1,0:T(8,128)(2,1)S(1)}, u32[]{:S(2)}, u32[]{:S(2)}) async-start(bf16[16,1,12,2048]{3,2,1,0:T(8,128)(2,1)} %bitcast.30), calls=%async_computation.2 | async-start | bytes 2097152 | tf_op jit(solution)/shard_map/all_to_all | solution.py:80
  30.3 6.5 %scatter_custom_fusion.1 = bf16[192,2048]{1,0:T(8,128)(2,1)S(1)} fusion(s32[1024]{0:T(1024)S(1)} %bitcast.258, bf16[128,2048]{1,0:T(8,128)(2,1)S(1)} %copy-done.5, bf16[]{:T(256)} %constant.43.clone.1), kind=kCustom, calls=%fused_computation.25 | custom fusion | bytes 1310722 | tf_op jit(solution)/shard_map/scatter | solution.py:75
  36.8 1.1 reshape.389
  37.9 15.2 %all-to-all-done.2 = bf16[16,1,12,2048]{3,2,1,0:T(8,128)(2,1)S(1)} async-done(((bf16[16,1,12,2048]{3,2,1,0:T(8,128)(2,1)}), bf16[16,1,12,2048]{3,2,1,0:T(8,128)(2,1)S(1)}, u32[]{:S(2)}, u32[]{:S(2)}) %all-to-all-start.2) | async-done | bytes 786464 | tf_op jit(solution)/shard_map/all_to_all | solution.py:80
  53.1 6.8 %all-to-all-start.1 = ((bf16[16,1,12,2048]{3,2,1,0:T(8,128)(2,1)}), bf16[16,1,12,2048]{3,2,1,0:T(8,128)(2,1)}, u32[]{:S(2)}, u32[]{:S(2)}) async-start(bf16[16,1,12,2048]{3,2,1,0:T(8,128)(2,1)} %bitcast.14), calls=%async_computation.1 | async-start | bytes 2097152 | tf_op jit(solution)/shard_map/all_to_all | solution.py:79
  60.0 0.2 all-gather.11.cloned.1.call-start
  60.2 0.3 all-gather.11.cloned.1.call-update
  60.6 0.1 copy.54
  60.9 6.9 %scatter_custom_fusion = bf16[192,2048]{1,0:T(8,128)(2,1)S(1)} fusion(s32[1024]{0:T(1024)S(1)} %bitcast.259, f32[128,2048]{1,0:T(8,128)S(1)} %convert_element_type.84, f32[1024]{0:T(1024)S(1)} %mul.184, bf16[]{:T(256)} %constant.43.clone.1), kind=kCustom, calls=%fused_computation.22 | custom fusion | flops 4194304 | bytes 1839106 | tf_op jit(solution)/shard_map/scatter | solution.py:77
  67.8 1.1 reshape.385
  69.0 13.9 %all-to-all-done.1 = bf16[16,1,12,2048]{3,2,1,0:T(8,128)(2,1)} async-done(((bf16[16,1,12,2048]{3,2,1,0:T(8,128)(2,1)}), bf16[16,1,12,2048]{3,2,1,0:T(8,128)(2,1)}, u32[]{:S(2)}, u32[]{:S(2)}) %all-to-all-start.1) | async-done | bytes 786464 | tf_op jit(solution)/shard_map/all_to_all | solution.py:79
  82.9 6.8 %all-to-all-start = ((bf16[16,1,12,2048]{3,2,1,0:T(8,128)(2,1)}), bf16[16,1,12,2048]{3,2,1,0:T(8,128)(2,1)S(1)}, u32[]{:S(2)}, u32[]{:S(2)}) async-start(bf16[16,1,12,2048]{3,2,1,0:T(8,128)(2,1)} %bitcast.6), calls=%async_computation | async-start | bytes 2097152 | tf_op jit(solution)/shard_map/all_to_all | solution.py:81
  89.8 2.9 all-gather.9.cloned.1.call-done
  92.7 6.4 %fusion.44 = f32[16,1,12,2,768]{4,0,2,3,1:T(8,128)} fusion(bf16[1,2,768,2048]{3,2,1,0:T(8,128)(2,1)} %all-gather.9.cloned.1.call-done, bf16[16,1,12,2048]{3,2,1,0:T(8,128)(2,1)} %all-to-all-done.1), kind=kOutput, calls=%fused_computation.41 | convolution fusion | flops 1207959552 | bytes 8257536 | tf_op jit(solution)/shard_map/nesd,egfd->nesgf/dot_general | solution.py:17
  99.1 75.5 %all-gather.13.cloned.1.call-done = bf16[1,2,768,2048]{3,2,1,0:T(8,128)(2,1)} async-done(((bf16[1,2,768,1024]{3,2,1,0:T(8,128)(2,1)}), bf16[1,2,768,2048]{3,2,1,0:T(8,128)(2,1)}) %all-gather.13.cloned.1.call-update) | async-done | bytes 6291472 | tf_op jit(solution)/shard_map/all_gather | solution.py:56
  174.6 5.5 %fusion.6 = f32[16,12,2,768]{3,0,1,2:T(8,128)S(1)} fusion(bf16[1,2,768,2048]{3,2,1,0:T(8,128)(2,1)} %all-gather.13.cloned.1.call-done, bf16[16,1,12,2048]{3,2,1,0:T(8,128)(2,1)} %all-to-all-done.1), kind=kOutput, calls=%fused_computation.14 | convolution fusion | flops 1207959552 | bytes 8257536 | tf_op jit(solution)/shard_map/nesd,egfd->nesgf/dot_general | solution.py:19
  180.1 3.3 fusion.50
  183.5 4.9 %fusion.26 = bf16[1,768,2048]{2,1,0:T(8,128)(2,1)} fusion(bf16[16,1,12,2048]{3,2,1,0:T(8,128)(2,1)S(1)} %all-to-all-done, f32[16,1,12,2,768]{4,0,2,3,1:T(8,128)} %fusion.50, f32[16,1,12,2,768]{4,0,2,3,1:T(8,128)} %fusion.44), kind=kOutput, calls=%fused_computation.33 | convolution fusion | flops 607469568 | bytes 6291456 | tf_op jit(solution)/shard_map/nesf,nesd->efd/dot_general | solution.py:41
  188.4 32.7 %all-gather.7.cloned.1.call-done = bf16[1,768,2048]{2,1,0:T(8,128)(2,1)} async-done(((bf16[1,768,1024]{2,1,0:T(8,128)(2,1)}), bf16[1,768,2048]{2,1,0:T(8,128)(2,1)}) %all-gather.7.cloned.1.call-update) | async-done | bytes 3145744 | tf_op jit(solution)/shard_map/all_gather | solution.py:58
  221.1 3.3 fusion.53
  224.4 43.0 %all-gather.11.cloned.1.call-done = bf16[1,768,2048]{2,1,0:T(8,128)(2,1)} async-done(((bf16[1,768,1024]{2,1,0:T(8,128)(2,1)}), bf16[1,768,2048]{2,1,0:T(8,128)(2,1)}) %all-gather.11.cloned.1.call-update) | async-done | bytes 3145744 | tf_op jit(solution)/shard_map/all_gather | solution.py:57
  267.4 4.5 fusion.94
  272.0 4.5 fusion.27
  276.6 1.5 fusion.39
  278.1 1.6 copy.63
  279.8 5.6 %all-to-all-start.3 = ((bf16[16,1,12,2048]{3,2,1,0:T(8,128)(2,1)}), bf16[16,1,12,2048]{3,2,1,0:T(8,128)(2,1)S(1)}, u32[]{:S(2)}, u32[]{:S(2)}) async-start(bf16[16,1,12,2048]{3,2,1,0:T(8,128)(2,1)} %copy.63), calls=%async_computation.3 | async-start | bytes 2097152 | tf_op jit(solution)/shard_map/all_to_all | solution.py:86
  285.6 22.6 %all-to-all-done.3 = bf16[16,1,12,2048]{3,2,1,0:T(8,128)(2,1)S(1)} async-done(((bf16[16,1,12,2048]{3,2,1,0:T(8,128)(2,1)}), bf16[16,1,12,2048]{3,2,1,0:T(8,128)(2,1)S(1)}, u32[]{:S(2)}, u32[]{:S(2)}) %all-to-all-start.3) | async-done | bytes 786464 | tf_op jit(solution)/shard_map/all_to_all | solution.py:86
  308.2 0.2 reshape.400
  308.4 6.9 %gather_fusion = f32[1024,2048]{1,0:T(8,128)} fusion(f32[192,2048]{1,0:T(8,128)S(1)} %reshape.400, s32[1024]{0:T(1024)S(1)} %broadcast_clamp_fusion), kind=kCustom, calls=%fused_computation | custom fusion | bytes 16781312 | tf_op jit(solution)/shard_map/gather | solution.py:90
  315.2 7.8 %fusion.1 = bf16[128,2048]{1,0:T(8,128)(2,1)} fusion(f32[1024,2048]{1,0:T(8,128)} %gather_fusion, pred[128,8]{1,0:T(8,128)(4,1)S(1)} %fusion.99), kind=kLoop, calls=%fused_computation.7 | loop fusion | flops 3932160 | bytes 8913920 | tf_op jit(solution)/shard_map/reduce_sum | solution.py:92
  323.1 1.9 fusion.59
  325.1 6.0 %fusion.3 = bf16[1,2,768,2048]{3,2,1,0:T(8,128)(2,1)} fusion(f32[2,768,2048,1]{2,1,3,0:T(8,128)S(1)} %fusion.59, bf16[16,12,1,768]{3,0,1,2:T(8,128)(2,1)S(1)} %copy-done.12, bf16[16,12,1,768]{3,0,1,2:T(8,128)(2,1)S(1)} %copy-done.14, bf16[16,1,12,2048]{3,2,1,0:T(8,128)(2,1)} %all-to-all-done.1), kind=kOutput, calls=%fused_computation.10 | convolution fusion | flops 1214545920 | bytes 20250624 | tf_op jit(solution)/shard_map/nesd,nesgf->egfd/dot_general | solution.py:40
  331.2 3.6 convert_element_type.101
  334.7 62.4 %all-gather.15.cloned.1.call-done = bf16[1024,2048]{1,0:T(8,128)(2,1)} async-done(((bf16[128,2048]{1,0:T(8,128)(2,1)}), bf16[1024,2048]{1,0:T(8,128)(2,1)}) %all-gather.15.cloned.1.call-update) | async-done | bytes 4194320 | tf_op jit(solution)/shard_map/all_gather | solution.py:9
  397.2 3.0 reduce_sum.32
  400.1 1.1 convert_element_type.93
  401.2 74.5 %reduce-scatter.3.cloned.1.call-done = bf16[1,2,768,1024]{3,2,1,0:T(8,128)(2,1)} async-done(((bf16[1,2,768,2048]{3,2,1,0:T(8,128)(2,1)}), bf16[1,2,768,1024]{3,2,1,0:T(8,128)(2,1)}) %reduce-scatter.3.cloned.1.call-update) | async-done | bytes 3145744 | tf_op jit(solution)/shard_map/reduce_scatter | solution.py:95
  475.8 5.3 %convert_element_type.96 = f32[1,2,768,1024]{3,2,1,0:T(8,128)} convert(bf16[1,2,768,1024]{3,2,1,0:T(8,128)(2,1)} %reduce-scatter.3.cloned.1.call-done) | non-fusion elementwise | flops 1572864 | bytes 9437184 | tf_op jit(solution)/shard_map/convert_element_type | solution.py:97
  (66 shorter events, 1.4 us)
Async XLA Ops:
  7.2 7.8 %copy-start = (bf16[128,2048]{1,0:T(8,128)(2,1)S(1)}, bf16[128,2048]{1,0:T(8,128)(2,1)}, u32[]{:S(2)}) copy-start(bf16[128,2048]{1,0:T(8,128)(2,1)} %param.10) | copy-start | bytes 1572868
  7.2 2.2 copy-start.7
  7.2 85.5 %all-gather.9.cloned.1.call-start = ((), (), s32[]{:S(2)}) async-start(), calls=%async_computation.7 | async-start | bytes 9437184 | tf_op jit(solution)/shard_map/all_gather | solution.py:55
  7.9 166.7 %all-gather.13.cloned.1.call-start = ((), (), s32[]{:S(2)}) async-start(), calls=%async_computation.9 | async-start | bytes 9437184 | tf_op jit(solution)/shard_map/all_gather | solution.py:56
  8.7 21.6 %copy-start.5 = (bf16[128,2048]{1,0:T(8,128)(2,1)S(1)}, bf16[128,2048]{1,0:T(8,128)(2,1)}, u32[]{:S(2)}) copy-start(bf16[128,2048]{1,0:T(8,128)(2,1)} %param.9) | copy-start | bytes 1572868
  8.7 212.4 %all-gather.7.cloned.1.call-start = ((), (), s32[]{:S(2)}) async-start(), calls=%async_computation.6 | async-start | bytes 4718592 | tf_op jit(solution)/shard_map/all_gather | solution.py:58
  22.7 37.8 %copy-start.8 = (f32[128,8]{0,1:T(8,128)S(1)}, f32[128,8]{0,1:T(8,128)}, u32[]{:S(2)}) copy-start(f32[128,8]{0,1:T(8,128)} %param.13) | copy-start | bytes 12292
  22.7 38.1 %copy-start.6 = (bf16[128,2048]{1,0:T(8,128)(2,1)S(1)}, bf16[128,2048]{1,0:T(8,128)(2,1)}, u32[]{:S(2)}) copy-start(bf16[128,2048]{1,0:T(8,128)(2,1)} %param.11) | copy-start | bytes 1572868
  22.7 30.4 %all-to-all-start.2 = ((bf16[16,1,12,2048]{3,2,1,0:T(8,128)(2,1)}), bf16[16,1,12,2048]{3,2,1,0:T(8,128)(2,1)S(1)}, u32[]{:S(2)}, u32[]{:S(2)}) async-start(bf16[16,1,12,2048]{3,2,1,0:T(8,128)(2,1)} %bitcast.30), calls=%async_computation.2 | async-start | bytes 2097152 | tf_op jit(solution)/shard_map/all_to_all | solution.py:80
  53.1 127.0 %copy-start.3 = (bf16[16,1,12,2048]{3,2,1,0:T(8,128)(2,1)}, bf16[16,1,12,2048]{3,2,1,0:T(8,128)(2,1)S(1)}, u32[]{:S(2)}) copy-start(bf16[16,1,12,2048]{3,2,1,0:T(8,128)(2,1)S(1)} %all-to-all-done.2) | copy-start | bytes 2359300
  53.1 29.8 %all-to-all-start.1 = ((bf16[16,1,12,2048]{3,2,1,0:T(8,128)(2,1)}), bf16[16,1,12,2048]{3,2,1,0:T(8,128)(2,1)}, u32[]{:S(2)}, u32[]{:S(2)}) async-start(bf16[16,1,12,2048]{3,2,1,0:T(8,128)(2,1)} %bitcast.14), calls=%async_computation.1 | async-start | bytes 2097152 | tf_op jit(solution)/shard_map/all_to_all | solution.py:79
  60.0 207.4 %all-gather.11.cloned.1.call-start = ((), (), s32[]{:S(2)}) async-start(), calls=%async_computation.8 | async-start | bytes 4718592 | tf_op jit(solution)/shard_map/all_gather | solution.py:57
  82.9 100.5 %all-to-all-start = ((bf16[16,1,12,2048]{3,2,1,0:T(8,128)(2,1)}), bf16[16,1,12,2048]{3,2,1,0:T(8,128)(2,1)S(1)}, u32[]{:S(2)}, u32[]{:S(2)}) async-start(bf16[16,1,12,2048]{3,2,1,0:T(8,128)(2,1)} %bitcast.6), calls=%async_computation | async-start | bytes 2097152 | tf_op jit(solution)/shard_map/all_to_all | solution.py:81
  89.7 241.4 %reduce-scatter.5.cloned.1.call-start = ((), (), s32[]{:S(2)}) async-start(), calls=%async_computation.11 | async-start | bytes 4718592 | tf_op jit(solution)/shard_map/reduce_scatter | solution.py:98
  174.6 5.5 %copy-start.2 = (bf16[1,2,768,2048]{3,2,1,0:T(8,128)(2,1)S(1)}, bf16[1,2,768,2048]{3,2,1,0:T(8,128)(2,1)}, u32[]{:S(2)}) copy-start(bf16[1,2,768,2048]{3,2,1,0:T(8,128)(2,1)} %all-gather.9.cloned.1.call-done) | copy-start | bytes 18874372
  267.4 9.1 %slice-start = ((s8[6291456]{0:T(1024)(128)(4,1)}), s8[2097152]{0:T(1024)(128)(4,1)S(1)}, s32[]{:S(2)}) async-start(s8[6291456]{0:T(1024)(128)(4,1)} %bitcast.260), calls=%async_computation.13 | async-start | bytes 4194304
  272.0 4.6 copy-start.11
  272.0 4.6 copy-start.13
  272.0 4.6 copy-start.9
  272.0 4.7 slice-start.1
  279.8 28.4 %all-to-all-start.3 = ((bf16[16,1,12,2048]{3,2,1,0:T(8,128)(2,1)}), bf16[16,1,12,2048]{3,2,1,0:T(8,128)(2,1)S(1)}, u32[]{:S(2)}, u32[]{:S(2)}) async-start(bf16[16,1,12,2048]{3,2,1,0:T(8,128)(2,1)} %copy.63), calls=%async_computation.3 | async-start | bytes 2097152 | tf_op jit(solution)/shard_map/all_to_all | solution.py:86
  285.3 111.9 %all-gather.15.cloned.1.call-start = ((), (), s32[]{:S(2)}) async-start(), calls=%async_computation.12 | async-start | bytes 4718592 | tf_op jit(solution)/shard_map/all_gather | solution.py:9
  315.2 7.9 %copy-start.4 = (bf16[16,1,12,2048]{3,2,1,0:T(8,128)(2,1)S(1)}, bf16[16,1,12,2048]{3,2,1,0:T(8,128)(2,1)}, u32[]{:S(2)}) copy-start(bf16[16,1,12,2048]{3,2,1,0:T(8,128)(2,1)} %copy-done.3) | copy-start | bytes 2359300
  315.2 7.9 %copy-start.10 = (bf16[16,12,1,768]{3,0,1,2:T(8,128)(2,1)S(1)}, bf16[16,12,1,768]{3,0,1,2:T(8,128)(2,1)}, u32[]{:S(2)}) copy-start(bf16[16,12,1,768]{3,0,1,2:T(8,128)(2,1)} %copy-done.9) | copy-start | bytes 884740
  323.0 2.0 copy-start.12
  323.0 2.0 copy-start.14
  323.0 152.7 %reduce-scatter.3.cloned.1.call-start = ((), (), s32[]{:S(2)}) async-start(), calls=%async_computation.10 | async-start | bytes 9437184 | tf_op jit(solution)/shard_map/reduce_scatter | solution.py:95
  400.1 81.0 %copy-start.1 = (bf16[128,2048]{1,0:T(8,128)(2,1)S(1)}, bf16[128,2048]{1,0:T(8,128)(2,1)}, u32[]{:S(2)}) copy-start(bf16[128,2048]{1,0:T(8,128)(2,1)} %param.10) | copy-start | bytes 1572868
Sparse Core Ops, SparseCore 0:
  9.5 83.0 all-gather.8
  94.2 80.3 all-gather.12
  176.1 44.8 all-gather.6
  222.5 44.8 all-gather.10
  270.1 43.4 reduce-scatter.4
  323.1 73.9 all-gather.14
  400.0 75.6 reduce-scatter.2
